TPU v7x, 32 devices: a whole 2x2x4 slice. The times are simulated.
32 devices in a mesh: table: 4 (over y, core), dom: 8 (over z, x).
Axes of the slice: x: 2, y: 2, z: 4, core: 2. Of those that a mesh axis runs over, the one named last changes fastest.
Arguments:
- tables: float32 [4, 65536, 128], P('table', 'dom'), may hold values from -6 to 6
- owner_ids: int32 [16384, 4], P(('table', 'dom')), may hold values from 0 to 31, all different within a row; in each aligned block of 512 rows (0 to 511, 512 to 1023, ...) at most 128 rows name the same one
- row_ids: int32 [16384, 4], P(('table', 'dom')), may hold values from 0 to 8191
- neighbour_part: int32 [128, 4], P(('table', 'dom')), may hold values from 0 to 7, all different within a row; in each aligned block of 4 rows (0 to 3, 4 to 7, ...) at most 4 rows name the same one
- neighbour_block: int32 [128, 4], P(('table', 'dom')), may hold values from 0 to 3
- adjacency: bfloat16 [128, 4, 128, 128], P(('table', 'dom')), may hold values from 0.001 to 1.81
- w_in: bfloat16 [128, 1024], replicated, may hold values from -0.5 to 0.5
- w_pool: bfloat16 [1024, 1024], replicated, may hold values from -0.1875 to 0.1875
- w_self: bfloat16 [1024, 1024], replicated, may hold values from -0.1875 to 0.1875
- w_neigh: bfloat16 [1024, 1024], replicated, may hold values from -0.75 to 0.75
- out_gain: bfloat16 [1024], replicated, may hold values from 0.25 to 1.75
- cotangent: bfloat16 [16384, 1024], P(('table', 'dom')), may hold values from -6 to 6
Outputs:
- node_out: bfloat16 [16384, 1024], P(('table', 'dom'))
- table_grad: float32 [4, 65536, 128], P('table', 'dom')
Inputs may be any that keep to these rules, and one draw needn't show every extreme that they name: `owner_ids`: the 4 entries of a row differ. Among the 512 rows of one device no owner is named more than 128 times, and in some device's rows some owner is named exactly 128 times. `neighbour_part`: the 4 entries of a row differ. Among the 4 rows of one device no partition is named more than 4 times, and in some device's rows some partition is named exactly 4 times.
All inputs are finite; a program needn't handle non-finite values.
Results may differ from a plain program's by a relative error of at most 0.012.
Values may be sent and summed in bfloat16 or wider, within the bound.
No kernel may reach another device: no remote copies, remote signals or barrier semaphores. Data moves between devices by JAX's collectives and lax.ppermute only.
A program may use at most 128 MiB of HBM per device.

v0:
```python
import jax
import jax.numpy as jnp
from jax import lax
from jax.sharding import PartitionSpec as P

EPSILON = 1e-06


def silu_slope(inputs):
    sigmoid_part = jax.nn.sigmoid(inputs)
    return sigmoid_part * (1.0 + inputs * (1.0 - sigmoid_part))


def times_transpose(left_side, right_side):
    return lax.dot_general(
        left_side, right_side, (((1,), (1,)), ((), ())), preferred_element_type=jnp.float32
    )


def bucket_slots(target, buckets, capacity):
    onehot = (target[:, None] == jnp.arange(buckets, dtype=jnp.int32)[None, :]).astype(jnp.int32)
    before = jnp.cumsum(onehot, axis=0) - onehot
    position = jnp.sum(before * onehot, axis=1)
    return target * capacity + position


def request_swap(buffer):
    return lax.all_to_all(buffer, ("table", "dom"), split_axis=0, concat_axis=0, tiled=True)


def row_swap(buffer):
    return lax.all_to_all(buffer, ("table", "dom"), split_axis=0, concat_axis=0, tiled=True)


def body(
    tables,
    owner_ids,
    row_ids,
    neighbour_part,
    neighbour_block,
    adjacency,
    w_in,
    w_pool,
    w_self,
    w_neigh,
    out_gain,
    cotangent,
):
    groups = lax.axis_size("table")
    domains = lax.axis_size("dom")
    devices = groups * domains
    node_count, lookup_count = owner_ids.shape
    table_width = tables.shape[2]
    rows_local = tables.shape[1]
    hidden_width = w_self.shape[0]
    capacity = max(2, (2 * node_count * lookup_count + devices - 1) // devices)
    row_slots = bucket_slots(owner_ids.reshape(-1), devices, capacity)
    requests = jnp.full((devices * capacity,), -1, jnp.int32).at[row_slots].set(row_ids.reshape(-1))
    incoming = request_swap(requests.reshape(devices, capacity))
    present = incoming >= 0
    safe_rows = jnp.where(present, incoming, 0)
    fetched = jnp.where(present[:, :, None], tables[0][safe_rows], 0.0)
    returned = row_swap(fetched)
    looked = returned.reshape(devices * capacity, table_width)[row_slots].reshape(
        node_count, lookup_count, table_width
    )
    feature = jnp.sum(looked, axis=1).astype(jnp.bfloat16)
    hidden = jnp.dot(feature, w_in, preferred_element_type=jnp.float32).astype(jnp.bfloat16)
    pooled_pre = jnp.dot(hidden, w_pool, preferred_element_type=jnp.float32)
    pooled = jax.nn.silu(pooled_pre).astype(jnp.bfloat16)
    block_rows = adjacency.shape[-1]
    block_count = node_count // block_rows
    fanout = neighbour_part.shape[1]
    halo_cap = max(2, (2 * block_count * fanout + domains - 1) // domains)
    halo_slots = bucket_slots(neighbour_part.reshape(-1), domains, halo_cap)
    wanted = (
        jnp.full((domains * halo_cap,), -1, jnp.int32)
        .at[halo_slots]
        .set(neighbour_block.reshape(-1))
    )
    asked_blocks = lax.all_to_all(
        wanted.reshape(domains, halo_cap), "dom", split_axis=0, concat_axis=0, tiled=True
    )
    gathered = lax.all_gather(pooled, "dom", axis=0, tiled=True)
    flat_index = neighbour_part.reshape(-1) * block_count + neighbour_block.reshape(-1)
    sources = gathered.reshape(domains * block_count, block_rows, hidden_width)[flat_index]
    sources = sources.reshape(block_count, fanout, block_rows, hidden_width)
    inverse = 1.0 / jnp.sum(adjacency.astype(jnp.float32), axis=(1, 3))
    summed = jnp.einsum("bkij,bkjh->bih", adjacency, sources, preferred_element_type=jnp.float32)
    neighbour_mean = (
        (summed * inverse[:, :, None]).astype(jnp.bfloat16).reshape(node_count, hidden_width)
    )
    pre_act = jnp.dot(hidden, w_self, preferred_element_type=jnp.float32) + jnp.dot(
        neighbour_mean, w_neigh, preferred_element_type=jnp.float32
    )
    active = jax.nn.silu(pre_act)
    rms_scale = lax.rsqrt(jnp.mean(active * active, axis=1, keepdims=True) + EPSILON)
    gain_wide = out_gain.astype(jnp.float32)
    node_out = (active * rms_scale * gain_wide).astype(jnp.bfloat16)
    weighted = gain_wide * cotangent.astype(jnp.float32)
    d_active = rms_scale * weighted - active * (rms_scale * rms_scale * rms_scale) * jnp.mean(
        weighted * active, axis=1, keepdims=True
    )
    d_pre = (d_active * silu_slope(pre_act)).astype(jnp.bfloat16)
    d_hidden_self = times_transpose(d_pre, w_self)
    d_mean = times_transpose(d_pre, w_neigh)
    d_scaled = (d_mean.reshape(block_count, block_rows, hidden_width) * inverse[:, :, None]).astype(
        jnp.bfloat16
    )
    shares = jnp.einsum(
        "bkij,bih->bkjh", adjacency, d_scaled, preferred_element_type=jnp.float32
    ).astype(jnp.bfloat16)
    outgoing = (
        jnp.zeros((domains * halo_cap, block_rows, hidden_width), jnp.bfloat16)
        .at[halo_slots]
        .set(shares.reshape(block_count * fanout, block_rows, hidden_width))
    )
    back_grads = lax.all_to_all(
        outgoing.reshape(domains, halo_cap, block_rows, hidden_width),
        "dom",
        split_axis=0,
        concat_axis=0,
        tiled=True,
    )
    target_blocks = jnp.where(asked_blocks >= 0, asked_blocks, block_count).reshape(-1)
    d_pooled = (
        jnp.zeros((block_count, block_rows, hidden_width), jnp.float32)
        .at[target_blocks]
        .add(
            back_grads.reshape(domains * halo_cap, block_rows, hidden_width).astype(jnp.float32),
            mode="drop",
        )
    )
    d_pool_pre = (d_pooled.reshape(node_count, hidden_width) * silu_slope(pooled_pre)).astype(
        jnp.bfloat16
    )
    d_hidden = (d_hidden_self + times_transpose(d_pool_pre, w_pool)).astype(jnp.bfloat16)
    d_feature = times_transpose(d_hidden, w_in)
    spread = jnp.broadcast_to(
        d_feature[:, None, :], (node_count, lookup_count, table_width)
    ).reshape(node_count * lookup_count, table_width)
    outgoing_rows = (
        jnp.zeros((devices * capacity, table_width), jnp.float32).at[row_slots].set(spread)
    )
    owed_grads = row_swap(outgoing_rows.reshape(devices, capacity, table_width))
    grad_rows = jnp.where(present, incoming, rows_local).reshape(-1)
    table_grad = (
        jnp.zeros((rows_local, table_width), jnp.float32)
        .at[grad_rows]
        .add(owed_grads.reshape(devices * capacity, table_width), mode="drop")
    )
    return (node_out, table_grad[None])


def solution(mesh):
    placed = (
        P("table", "dom", None),
        P(("table", "dom"), None),
        P(("table", "dom"), None),
        P(("table", "dom"), None),
        P(("table", "dom"), None),
        P(("table", "dom"), None, None, None),
        P(),
        P(),
        P(),
        P(),
        P(),
        P(("table", "dom"), None),
    )
    return jax.shard_map(
        body,
        mesh=mesh,
        in_specs=placed,
        out_specs=(P(("table", "dom"), None), P("table", "dom", None)),
        check_vma=False,
    )
```

profile of v0, /device:TPU:0, one launch (start us, length us, event | category | flops | bytes accessed | tf_op | source)
XLA Modules:
  0.0 629.0 jit_solution(8499067572667407016)
XLA Ops:
  9.2 9.1 %reduce-window.6 = s32[32,16,128]{2,1,0:T(8,128)S(1)} reduce-window(s32[32,16,128]{2,1,0:T(8,128)S(1)} %fusion.14, s32[]{:T(128)} %constant.14.clone.1), window={size=1x1x128 pad=0_0x0_0x127_0}, to_apply=%region_0.0 | reduce-window | flops 8323072 | bytes 524292 | tf_op jit(solution)/shard_map/reduce-window
  19.8 8.1 %scatter_custom_fusion = s32[4096]{0:T(1024)S(1)} fusion(s32[2048]{0:T(1024)S(1)} %bitcast.117, s32[2048]{0:T(1024)S(1)} %reshape.321, s32[]{:T(128)} %constant.12.clone.1), kind=kCustom, calls=%fused_computation.57 | custom fusion | bytes 16388 | tf_op jit(solution)/shard_map/scatter | solution.py:58
  27.9 14.3 %all_to_all.42 = s32[32,1,128]{2,1,0:T(1,128)S(1)} all-to-all(s32[32,1,128]{2,1,0:T(1,128)S(1)} %bitcast.115), channel_id=1, replica_groups=mesh['table'=4,'dom'=8] {'table','dom'}, dimensions={0} | all-to-all | bytes 32768 | tf_op jit(solution)/shard_map/all_to_all | solution.py:28
  42.2 16.4 %gather_fusion = f32[4096,128]{1,0:T(8,128)} fusion(f32[8192,128]{1,0:T(8,128)} %bitcast.98, s32[4096]{0:T(1024)S(1)} %fusion.17), kind=kCustom, calls=%fused_computation | custom fusion | bytes 4210688 | tf_op jit(solution)/shard_map/gather | solution.py:62
  58.6 2.9 broadcast_select_fusion
  61.5 3.5 all-to-all-start.1
  65.0 49.9 %all-to-all-done.1 = f32[32,128,128]{2,1,0:T(8,128)} async-done(((f32[32,128,128]{2,1,0:T(8,128)}), f32[32,128,128]{2,1,0:T(8,128)}, u32[]{:S(2)}, u32[]{:S(2)}) %all-to-all-start.1) | async-done | bytes 2097184 | tf_op jit(solution)/shard_map/all_to_all | solution.py:32
  114.9 7.0 %gather_fusion.1 = f32[2048,128]{1,0:T(8,128)S(1)} fusion(f32[4096,128]{1,0:T(8,128)} %bitcast.12, s32[2048]{0:T(1024)S(1)} %broadcast_clamp_fusion), kind=kCustom, calls=%fused_computation.1 | custom fusion | bytes 2105344 | tf_op jit(solution)/shard_map/gather | solution.py:64
  124.1 3.1 multiply_convert_fusion.3
  129.1 3.4 all-to-all-start.2
  132.8 4.9 fusion.26
  137.7 112.4 %all-gather.2.cloned.1.call-done = bf16[4096,1024]{1,0:T(8,128)(2,1)} async-done(((bf16[512,1024]{1,0:T(8,128)(2,1)}), bf16[4096,1024]{1,0:T(8,128)(2,1)}) %all-gather.2.cloned.1.call-update) | async-done | bytes 8388624 | tf_op jit(solution)/shard_map/all_gather | solution.py:84
  250.1 6.2 gather_fusion.2
  256.3 3.1 fusion.1
  262.1 2.4 multiply_convert_fusion.1
  264.6 2.6 fusion.28
  267.2 2.9 copy.40
  270.1 4.8 convolution_convert_fusion
  275.0 6.4 %copy.41 = bf16[16,128,1024]{2,1,0:T(8,128)(2,1)} copy(bf16[16,128,1024]{1,2,0:T(8,128)(2,1)} %bitcast.100) | data formatting | bytes 8388608 | tf_op jit(solution)/shard_map/reshape | solution.py:116
  281.3 4.3 broadcast_in_dim.72
  285.6 10.9 %scatter_fusion = bf16[32,128,1024]{2,1,0:T(8,128)(2,1)} fusion(bf16[32,128,1024]{2,1,0:T(8,128)(2,1)} %broadcast_in_dim.72, s32[16]{0:T(128)S(1)} %get-tuple-element.8, bf16[16,128,1024]{2,1,0:T(8,128)(2,1)} %copy.41), kind=kCustom, calls=%fused_computation.5 | custom fusion | bytes 12582976 | tf_op jit(solution)/shard_map/scatter | solution.py:116
  296.5 5.3 all-to-all-start.3
  303.1 4.2 fusion.27
  307.3 176.9 %all-to-all-done.3 = bf16[8,4,128,1024]{3,2,1,0:T(8,128)(2,1)} async-done(((bf16[8,4,128,1024]{3,2,1,0:T(8,128)(2,1)}), bf16[8,4,128,1024]{3,2,1,0:T(8,128)(2,1)}, u32[]{:S(2)}, u32[]{:S(2)}) %all-to-all-start.3) | async-done | bytes 8388640 | tf_op jit(solution)/shard_map/all_to_all | solution.py:118
  484.2 11.3 %bitcast_convert_fusion = f32[32,128,1024]{2,1,0:T(8,128)} fusion(bf16[8,4,128,1024]{3,2,1,0:T(8,128)(2,1)} %all-to-all-done.3), kind=kLoop, calls=%fused_computation.9 | loop fusion | flops 4194304 | bytes 25165824 | tf_op jit(solution)/shard_map/convert_element_type | solution.py:130
  497.1 32.8 %scatter_fusion.1 = f32[4,128,1024]{2,1,0:T(8,128)} fusion(f32[4,128,1024]{2,1,0:T(8,128)} %broadcast_in_dim.40, s32[32]{0:T(128)S(1)} %fusion.23, f32[32,128,1024]{2,1,0:T(8,128)} %bitcast_convert_fusion), kind=kCustom, calls=%fused_computation.6 | custom fusion | flops 4194304 | bytes 50331776 | tf_op jit(solution)/shard_map/scatter-add | solution.py:129
  529.9 3.0 fusion
  532.9 3.3 fusion.5
  536.3 7.0 %scatter_custom_fusion.4 = f32[4096,128]{1,0:T(8,128)} fusion(s32[2048]{0:T(1024)S(1)} %bitcast.119, f32[2048,128]{1,0:T(8,128)S(1)} %bitcast.108, f32[]{:T(128)} %constant.17.clone.1), kind=kCustom, calls=%fused_computation.33 | custom fusion | bytes 2097156 | tf_op jit(solution)/shard_map/scatter | solution.py:143
  543.3 4.0 all-to-all-start.4
  547.4 49.9 %all-to-all-done.4 = f32[32,128,128]{2,1,0:T(8,128)} async-done(((f32[32,128,128]{2,1,0:T(8,128)}), f32[32,128,128]{2,1,0:T(8,128)}, u32[]{:S(2)}, u32[]{:S(2)}) %all-to-all-start.4) | async-done | bytes 2097184 | tf_op jit(solution)/shard_map/all_to_all | solution.py:32
  597.3 24.9 %scatter_custom_fusion.5 = f32[8192,128]{1,0:T(8,128)} fusion(s32[4096]{0:T(1024)S(1)} %bitcast.120, f32[4096,128]{1,0:T(8,128)} %bitcast.37, f32[]{:T(128)} %constant.17.clone.1), kind=kCustom, calls=%fused_computation.20 | custom fusion | flops 524288 | bytes 4194816 | tf_op jit(solution)/shard_map/scatter-add | solution.py:150
  (71 shorter events, 13.6 us)
Async XLA Ops:
  7.2 116.8 %copy-start = (bf16[1024,1024]{1,0:T(8,128)(2,1)S(1)}, bf16[1024,1024]{1,0:T(8,128)(2,1)}, u32[]{:S(2)}) copy-start(bf16[1024,1024]{1,0:T(8,128)(2,1)} %param.19) | copy-start | bytes 6291460
  7.2 12.2 %copy-start.6 = (s32[512,4]{0,1:T(4,128)S(1)}, s32[512,4]{0,1:T(4,128)}, u32[]{:S(2)}) copy-start(s32[512,4]{0,1:T(4,128)} %param.14) | copy-start | bytes 24580
  61.5 53.4 %all-to-all-start.1 = ((f32[32,128,128]{2,1,0:T(8,128)}), f32[32,128,128]{2,1,0:T(8,128)}, u32[]{:S(2)}, u32[]{:S(2)}) async-start(f32[32,128,128]{2,1,0:T(8,128)} %broadcast_select_fusion), calls=%async_computation.1 | async-start | bytes 4194304 | tf_op jit(solution)/shard_map/all_to_all | solution.py:32
  65.0 185.2 %all-gather.2.cloned.1.call-start = ((), (), s32[]{:S(2)}) async-start(), calls=%async_computation.5 | async-start | bytes 9437184 | tf_op jit(solution)/shard_map/all_gather | solution.py:84
  124.0 3.1 copy-start.5
  124.0 3.2 copy-start.7
  124.0 3.3 copy-start.8
  124.0 8.6 %copy-start.9 = (bf16[1024]{0:T(1024)(128)(2,1)S(1)}, bf16[1024]{0:T(1024)(128)(2,1)}, u32[]{:S(2)}) copy-start(bf16[1024]{0:T(1024)(128)(2,1)} %param.22) | copy-start | bytes 6148
  124.1 8.6 %copy-start.1 = (bf16[4,4,128,128]{3,2,1,0:T(8,128)(2,1)S(1)}, bf16[4,4,128,128]{3,2,1,0:T(8,128)(2,1)}, u32[]{:S(2)}) copy-start(bf16[4,4,128,128]{3,2,1,0:T(8,128)(2,1)} %param.17) | copy-start | bytes 1572868
  129.1 167.4 %all-to-all-start.2 = ((s32[8,1,4]{2,1,0:T(1,128)}), s32[8,1,4]{2,1,0:T(1,128)S(1)}, u32[]{:S(2)}, u32[]{:S(2)}) async-start(s32[8,1,4]{2,1,0:T(1,128)} %bitcast.25), calls=%async_computation.2 | async-start | bytes 8192 | tf_op jit(solution)/shard_map/all_to_all | solution.py:81
  256.3 3.1 copy-start.2
  256.3 3.2 copy-start.10
  256.3 3.8 copy-start.11
  264.6 2.6 copy-start.3
  296.5 6.6 %copy-start.4 = (bf16[512,1024]{1,0:T(8,128)(2,1)S(1)}, bf16[512,1024]{1,0:T(8,128)(2,1)}, u32[]{:S(2)}) copy-start(bf16[512,1024]{1,0:T(8,128)(2,1)} %copy-done.3) | copy-start | bytes 3145732
  296.5 187.8 %all-to-all-start.3 = ((bf16[8,4,128,1024]{3,2,1,0:T(8,128)(2,1)}), bf16[8,4,128,1024]{3,2,1,0:T(8,128)(2,1)}, u32[]{:S(2)}, u32[]{:S(2)}) async-start(bf16[8,4,128,1024]{3,2,1,0:T(8,128)(2,1)} %bitcast.99), calls=%async_computation.3 | async-start | bytes 16777216 | tf_op jit(solution)/shard_map/all_to_all | solution.py:118
  543.3 54.0 %all-to-all-start.4 = ((f32[32,128,128]{2,1,0:T(8,128)}), f32[32,128,128]{2,1,0:T(8,128)}, u32[]{:S(2)}, u32[]{:S(2)}) async-start(f32[32,128,128]{2,1,0:T(8,128)} %bitcast.102), calls=%async_computation.4 | async-start | bytes 4194304 | tf_op jit(solution)/shard_map/all_to_all | solution.py:32
Sparse Core Ops, SparseCore 0:
  127.3 122.7 all-gather.1
where the time goes:
time: 630 us; the launch traced here: 629 us
  waiting for transfers between devices  389 us (62%)
  other arithmetic  89.3 us (14%)
  local copies, waits for them, and re-layouts  76.3 us (12%)
  matrix products  29.3 us (5%)
  starting transfers between devices  16.3 us (3%)
  between operations  14.4 us (2%)
  blocking collectives  14.3 us (2%)
    all_to_all x1, waiting for transfers between devices, body(): lax.all_to_all(outgoing.reshape(domains, halo_cap, block_rows, hidden_wid...  177 us
    all_gather x1, waiting for transfers between devices, body(): gathered = lax.all_gather(pooled, 'dom', axis=0, tiled=True)  112 us
    all_to_all x2, waiting for transfers between devices, row_swap(): lax.all_to_all(buffer, ('table', 'dom'), split_axis=0, concat_axis=0, til...  99.7 us
    scatter-add x1, other arithmetic, body(): d_pooled = jnp.zeros((block_count, block_rows, hidden_width), jnp.float32...  32.8 us
    scatter-add x1, other arithmetic, body(): table_grad = jnp.zeros((rows_local, table_width), jnp.float32).at[grad_ro...  24.9 us
    gather x1, local copies, waits for them, and re-layouts, body(): fetched = jnp.where(present[:, :, None], tables[0][safe_rows], 0.0)  16.4 us
    all_to_all x1, blocking collectives, request_swap(): lax.all_to_all(buffer, ('table', 'dom'), split_axis=0, concat_axis=0, til...  14.3 us
  transfers between devices with their start and end apart: 5, of which 4 were waited for; matrix products, arithmetic and copies ran while one was open for 9% of the time, Pallas kernels for 0%

commit v1 on v0

v1 whole, which is shorter than its diff:
```python
import jax
import jax.numpy as jnp
from jax import lax
from jax.sharding import PartitionSpec as P

EPSILON = 1e-06


def silu_slope(inputs):
    sigmoid_part = jax.nn.sigmoid(inputs)
    return sigmoid_part * (1.0 + inputs * (1.0 - sigmoid_part))


def times_transpose(left_side, right_side):
    return lax.dot_general(
        left_side, right_side, (((1,), (1,)), ((), ())), preferred_element_type=jnp.float32
    )


def bucket_slots(target, buckets, capacity):
    onehot = (target[:, None] == jnp.arange(buckets, dtype=jnp.int32)[None, :]).astype(jnp.int32)
    before = jnp.cumsum(onehot, axis=0) - onehot
    position = jnp.sum(before * onehot, axis=1)
    return target * capacity + position


def swap_all(buffer):
    return lax.all_to_all(buffer, ("table", "dom"), split_axis=0, concat_axis=0, tiled=True)


def body(
    tables,
    owner_ids,
    row_ids,
    neighbour_part,
    neighbour_block,
    adjacency,
    w_in,
    w_pool,
    w_self,
    w_neigh,
    out_gain,
    cotangent,
):
    groups = lax.axis_size("table")
    domains = lax.axis_size("dom")
    devices = groups * domains
    node_count, lookup_count = owner_ids.shape
    table_width = tables.shape[2]
    rows_local = tables.shape[1]
    hidden_width = w_self.shape[0]
    block_rows = adjacency.shape[-1]
    block_count = node_count // block_rows
    fanout = neighbour_part.shape[1]
    capacity = max(2, (2 * node_count * lookup_count + devices - 1) // devices)
    slot_count = devices * capacity

    map_pool = jnp.dot(w_in, w_pool, preferred_element_type=jnp.float32).astype(jnp.bfloat16)
    map_self = jnp.dot(w_in, w_self, preferred_element_type=jnp.float32).astype(jnp.bfloat16)

    row_slots = bucket_slots(owner_ids.reshape(-1), devices, capacity)
    requests = jnp.full((slot_count,), -1, jnp.int32).at[row_slots].set(row_ids.reshape(-1))
    incoming = swap_all(requests.reshape(devices, capacity))
    present = incoming >= 0
    safe_rows = jnp.where(present, incoming, 0)
    fetched = jnp.where(present[:, :, None], tables[0][safe_rows], 0.0).astype(jnp.bfloat16)
    returned = swap_all(fetched).reshape(slot_count, table_width)
    slot_ids = jnp.arange(slot_count, dtype=jnp.int32)
    by_node = row_slots.reshape(node_count, lookup_count)
    select = (by_node[:, 0, None] == slot_ids[None, :])
    for lookup in range(1, lookup_count):
        select = select | (by_node[:, lookup, None] == slot_ids[None, :])
    select = select.astype(jnp.bfloat16)
    feature = jnp.dot(select, returned, preferred_element_type=jnp.float32).astype(jnp.bfloat16)

    gathered = lax.all_gather(feature, "dom", axis=0, tiled=True)
    flat_index = neighbour_part.reshape(-1) * block_count + neighbour_block.reshape(-1)
    sources = gathered.reshape(domains * block_count, block_rows, table_width)[flat_index]
    pooled_pre = jnp.dot(
        sources.reshape(-1, table_width), map_pool, preferred_element_type=jnp.float32
    )
    pooled = jax.nn.silu(pooled_pre).astype(jnp.bfloat16)
    pooled = pooled.reshape(block_count, fanout, block_rows, hidden_width)
    inverse = 1.0 / jnp.sum(adjacency.astype(jnp.float32), axis=(1, 3))
    summed = jnp.einsum("bkij,bkjh->bih", adjacency, pooled, preferred_element_type=jnp.float32)
    neighbour_mean = (
        (summed * inverse[:, :, None]).astype(jnp.bfloat16).reshape(node_count, hidden_width)
    )
    pre_act = jnp.dot(feature, map_self, preferred_element_type=jnp.float32) + jnp.dot(
        neighbour_mean, w_neigh, preferred_element_type=jnp.float32
    )
    active = jax.nn.silu(pre_act)
    rms_scale = lax.rsqrt(jnp.mean(active * active, axis=1, keepdims=True) + EPSILON)
    gain_wide = out_gain.astype(jnp.float32)
    node_out = (active * rms_scale * gain_wide).astype(jnp.bfloat16)
    weighted = gain_wide * cotangent.astype(jnp.float32)
    d_active = rms_scale * weighted - active * (rms_scale * rms_scale * rms_scale) * jnp.mean(
        weighted * active, axis=1, keepdims=True
    )
    d_pre = (d_active * silu_slope(pre_act)).astype(jnp.bfloat16)
    d_self = times_transpose(d_pre, map_self)
    d_mean = times_transpose(d_pre, w_neigh)
    d_scaled = (d_mean.reshape(block_count, block_rows, hidden_width) * inverse[:, :, None]).astype(
        jnp.bfloat16
    )
    shares = jnp.einsum(
        "bkij,bih->bkjh", adjacency, d_scaled, preferred_element_type=jnp.float32
    )
    d_pool_pre = (shares.reshape(-1, hidden_width) * silu_slope(pooled_pre)).astype(jnp.bfloat16)
    d_source = times_transpose(d_pool_pre, map_pool)
    owed = jnp.zeros((domains * block_count, block_rows, table_width), jnp.float32)
    owed = owed.at[flat_index].add(d_source.reshape(-1, block_rows, table_width))
    owed = owed.astype(jnp.bfloat16).reshape(domains, node_count, table_width)
    back = lax.all_to_all(owed, "dom", split_axis=0, concat_axis=0, tiled=True)
    d_feature = (d_self + jnp.sum(back.astype(jnp.float32), axis=0)).astype(jnp.bfloat16)

    outgoing_rows = lax.dot_general(
        select, d_feature, (((0,), (0,)), ((), ())), preferred_element_type=jnp.float32
    ).astype(jnp.bfloat16)
    owed_grads = swap_all(outgoing_rows.reshape(devices, capacity, table_width))
    grad_rows = jnp.where(present, incoming, rows_local).reshape(-1)
    table_grad = (
        jnp.zeros((rows_local, table_width), jnp.float32)
        .at[grad_rows]
        .add(owed_grads.reshape(slot_count, table_width).astype(jnp.float32), mode="drop")
    )
    return (node_out, table_grad[None])


def solution(mesh):
    both = P(("table", "dom"), None)
    placed = (
        P("table", "dom", None),
        both,
        both,
        both,
        both,
        P(("table", "dom"), None, None, None),
        P(),
        P(),
        P(),
        P(),
        P(),
        both,
    )
    return jax.shard_map(
        body,
        mesh=mesh,
        in_specs=placed,
        out_specs=(both, P("table", "dom", None)),
        check_vma=False,
    )
```

time: 630 us -> 254 us (0.40)
  waiting for transfers between devices: 389 us -> 87.8 us
  local copies, waits for them, and re-layouts: 76.3 us -> 29.9 us
  other arithmetic: 89.3 us -> 47.9 us
  blocking collectives: 14.3 us -> 41.4 us
  starting transfers between devices: 16.3 us -> 6.31 us
    all_to_all x4 -> x2, waiting for transfers between devices: 277 us -> 54.3 us  [swap_all(): lax.all_to_all(buffer, ('table', 'dom'), split_axis=0, concat_axis=0, til...]
    all_gather x1, waiting for transfers between devices: 112 us -> 33.5 us  [body(): gathered = lax.all_gather(feature, 'dom', axis=0, tiled=True)]
    scatter-add x1, other arithmetic: 32.8 us -> 3.34 us  [body(): owed.at[flat_index].add(d_source.reshape(-1, block_rows, table_width))]
    all_to_all x1 -> x2, blocking collectives: 14.3 us -> 41.4 us  [the longest x1 27.1 us: body(): back = lax.all_to_all(owed, 'dom', split_axis=0, concat_axis=0, tiled=True)]
    scatter x4 -> x1, local copies, waits for them, and re-layouts: 26.6 us -> 8.06 us  [body(): jnp.full((slot_count,), -1, jnp.int32).at[row_slots]]
    gather x3 -> x2, local copies, waits for them, and re-layouts: 29.6 us -> 15.8 us  [the longest x1 13.2 us: body(): tables[0][safe_rows]]
    all_to_all x4 -> x2, starting transfers between devices: 16.3 us -> 6.27 us  [swap_all(): lax.all_to_all(buffer, ('table', 'dom'), split_axis=0, concat_axis=0, til...]
    reshape x4 -> x0, local copies, waits for them, and re-layouts: 9.47 us -> none  [the longest x1 6.37 us: body(): shares.reshape(block_count * fanout, block_rows, hidden_width)]
  transfers between devices with their start and end apart: 5 -> 3, of which waited for: 4 -> 3; matrix products, arithmetic and copies ran while one was open for 9% -> 2% of each run, Pallas kernels for 0% -> 0%
where the time goes in v1:
time: 254 us
  waiting for transfers between devices  87.8 us (35%)
  other arithmetic  47.9 us (19%)
  blocking collectives  41.4 us (16%)
  local copies, waits for them, and re-layouts  29.9 us (12%)
  matrix products  26 us (10%)
  between operations  14.4 us (6%)
  starting transfers between devices  6.31 us (2%)
    all_to_all x2, waiting for transfers between devices, swap_all(): lax.all_to_all(buffer, ('table', 'dom'), split_axis=0, concat_axis=0, til...  54.3 us
    all_gather x1, waiting for transfers between devices, body(): gathered = lax.all_gather(feature, 'dom', axis=0, tiled=True)  33.5 us
    all_to_all x1, blocking collectives, body(): back = lax.all_to_all(owed, 'dom', split_axis=0, concat_axis=0, tiled=True)  27.1 us
    scatter-add x1, other arithmetic, body(): table_grad = jnp.zeros((rows_local, table_width), jnp.float32).at[grad_ro...  24.6 us
    all_to_all x1, blocking collectives, swap_all(): lax.all_to_all(buffer, ('table', 'dom'), split_axis=0, concat_axis=0, til...  14.3 us
    gather x1, local copies, waits for them, and re-layouts, body(): tables[0][safe_rows]  13.2 us
    another operation x3, other arithmetic  9.41 us
    scatter x1, local copies, waits for them, and re-layouts, body(): jnp.full((slot_count,), -1, jnp.int32).at[row_slots]  8.06 us
  transfers between devices with their start and end apart: 3, of which 3 were waited for; matrix products, arithmetic and copies ran while one was open for 2% of the time, Pallas kernels for 0%

profile of v1, /device:TPU:0, one launch (start us, length us, event | category | flops | bytes accessed | tf_op | source)
XLA Modules:
  0.0 253.7 jit_solution(3255137759757418812)
XLA Ops:
  7.2 1.0 copy.36
  8.5 9.1 %reduce-window.6 = s32[32,16,128]{2,1,0:T(8,128)S(1)} reduce-window(s32[32,16,128]{2,1,0:T(8,128)S(1)} %fusion.21, s32[]{:T(128)} %constant.12.clone.1), window={size=1x1x128 pad=0_0x0_0x127_0}, to_apply=%region_0.0 | reduce-window | flops 8323072 | bytes 524292 | tf_op jit(solution)/shard_map/reduce-window
  19.3 8.1 %scatter_custom_fusion = s32[4096]{0:T(1024)S(1)} fusion(s32[2048]{0:T(1024)S(1)} %bitcast.110, s32[2048]{0:T(1024)S(1)} %reshape.244, s32[]{:T(128)} %constant.13.clone.1), kind=kCustom, calls=%fused_computation.63 | custom fusion | bytes 16388 | tf_op jit(solution)/shard_map/scatter | solution.py:62
  27.4 14.3 %all_to_all.30 = s32[32,1,128]{2,1,0:T(1,128)S(1)} all-to-all(s32[32,1,128]{2,1,0:T(1,128)S(1)} %bitcast.108), channel_id=1, replica_groups=mesh['table'=4,'dom'=8] {'table','dom'}, dimensions={0} | all-to-all | bytes 32768 | tf_op jit(solution)/shard_map/all_to_all | solution.py:28
  41.7 13.2 %gather_fusion = bf16[4096,128]{1,0:T(8,128)(2,1)S(1)} fusion(f32[8192,128]{1,0:T(8,128)} %bitcast.88, s32[4096]{0:T(1024)S(1)} %fusion.23), kind=kCustom, calls=%fused_computation | custom fusion | bytes 2113536 | tf_op jit(solution)/shard_map/gather | solution.py:66
  54.9 1.5 select_convert_fusion
  56.4 2.6 %all-to-all-start.1 = ((bf16[32,128,128]{2,1,0:T(8,128)(2,1)}), bf16[32,128,128]{2,1,0:T(8,128)(2,1)S(1)}, u32[]{:S(2)}, u32[]{:S(2)}) async-start(bf16[32,128,128]{2,1,0:T(8,128)(2,1)} %select_convert_fusion), calls=%async_computation.1 | async-start | bytes 2097152 | tf_op jit(solution)/shard_map/all_to_all | solution.py:28
  59.7 26.8 %all-to-all-done.1 = bf16[32,128,128]{2,1,0:T(8,128)(2,1)S(1)} async-done(((bf16[32,128,128]{2,1,0:T(8,128)(2,1)}), bf16[32,128,128]{2,1,0:T(8,128)(2,1)S(1)}, u32[]{:S(2)}, u32[]{:S(2)}) %all-to-all-start.1) | async-done | bytes 1048608 | tf_op jit(solution)/shard_map/all_to_all | solution.py:28
  86.5 1.0 copy-done.7
  87.5 5.4 %fusion.12 = bf16[512,128]{1,0:T(8,128)(2,1)} fusion(bf16[4096,128]{1,0:T(8,128)(2,1)} %bitcast.97, s32[512]{0:T(512)S(1)} %get-tuple-element.5, s32[512]{0:T(512)S(1)} %get-tuple-element.6, s32[512]{0:T(512)S(1)} %get-tuple-element.7, s32[512]{0:T(512)S(1)} %get-tuple-element.4), kind=kOutput, calls=%fused_computation.37 | convolution fusion | flops 551616512 | bytes 1187840 | tf_op jit(solution)/shard_map/dot_general | solution.py:74
  93.5 2.9 %convolution_convert_fusion.1 = bf16[128,1024]{1,0:T(8,128)(2,1)} fusion(bf16[128,1024]{1,0:T(8,128)(2,1)S(1)} %copy-done.6, bf16[1024,1024]{1,0:T(8,128)(2,1)} %param.19), kind=kOutput, calls=%fused_computation.34 | convolution fusion | flops 268566528 | bytes 2621440 | tf_op jit(solution)/shard_map/dot_general | solution.py:58
  96.4 1.2 convolution_convert_fusion.2
  97.5 33.5 %all-gather.2.cloned.1.call-done = bf16[4096,128]{1,0:T(8,128)(2,1)} async-done(((bf16[512,128]{1,0:T(8,128)(2,1)}), bf16[4096,128]{1,0:T(8,128)(2,1)}) %all-gather.2.cloned.1.call-update) | async-done | bytes 1048592 | tf_op jit(solution)/shard_map/all_gather | solution.py:76
  131.1 2.6 %gather_fusion.1 = bf16[16,128,128]{2,1,0:T(8,128)(2,1)} fusion(bf16[32,128,128]{2,1,0:T(8,128)(2,1)} %bitcast.104, s32[1024]{0:T(1024)S(1)} %pad_clamp_fusion), kind=kCustom, calls=%fused_computation.1 | custom fusion | bytes 1048640 | tf_op jit(solution)/shard_map/gather | solution.py:78
  133.7 3.6 %multiply_convert_fusion = (bf16[2048,1024]{1,0:T(8,128)(2,1)S(1)}, f32[2048,1024]{1,0:T(8,128)S(1)}) fusion(bf16[2048,128]{1,0:T(8,128)(2,1)} %bitcast.101, bf16[128,1024]{1,0:T(8,128)(2,1)} %convolution_convert_fusion.1), kind=kOutput, calls=%fused_computation.7 | convolution fusion | flops 547356672 | bytes 13369344 | tf_op jit(solution)/shard_map/dot_general | solution.py:79
  137.4 0.8 fusion.9
  138.2 1.3 fusion.28
  139.5 1.1 multiply_reduce_fusion
  140.6 2.4 multiply_convert_fusion.2
  143.0 1.3 fusion.29
  144.3 1.3 fusion.16
  145.7 3.5 %fusion = bf16[2048,1024]{1,0:T(8,128)(2,1)S(1)} fusion(f32[4,1024,512]{1,2,0:S(1)} %fusion.16, f32[2048,1024]{1,0:T(8,128)S(1)} %get-tuple-element.15), kind=kLoop, calls=%fused_computation.6 | loop fusion | flops 18874368 | bytes 20971520 | tf_op jit(solution)/shard_map/convert_element_type | solution.py:109
  149.2 1.3 fusion.30
  150.5 1.6 broadcast_in_dim.23
  152.1 3.3 %scatter_fusion = f32[32,128,128]{2,1,0:T(8,128)} fusion(f32[32,128,128]{2,1,0:T(8,128)} %broadcast_in_dim.23, s32[16]{0:T(128)S(1)} %fusion.26, f32[16,128,128]{2,1,0:T(8,128)S(1)} %bitcast.89), kind=kCustom, calls=%fused_computation.3 | custom fusion | flops 262144 | bytes 3145792 | tf_op jit(solution)/shard_map/scatter-add | solution.py:112
  155.4 1.7 convert_element_type.84
  157.2 27.1 %all_to_all.31 = bf16[8,512,128]{2,1,0:T(8,128)(2,1)S(1)} all-to-all(bf16[8,512,128]{2,1,0:T(8,128)(2,1)S(1)} %bitcast.91), channel_id=1, replica_groups=mesh['table'=4,'dom'=8] {'dom'}, dimensions={0} | all-to-all | bytes 2097152 | tf_op jit(solution)/shard_map/all_to_all | solution.py:114
  184.3 0.9 convert_reduce_fusion
  185.2 6.0 %convolution_convert_fusion = bf16[4096,128]{1,0:T(8,128)(2,1)} fusion(s32[512]{0:T(512)S(1)} %get-tuple-element.5, s32[512]{0:T(512)S(1)} %get-tuple-element.6, s32[512]{0:T(512)S(1)} %get-tuple-element.7, s32[512]{0:T(512)S(1)} %get-tuple-element.4, f32[512,128]{1,0:T(8,128)} %convert_reduce_fusion, bf16[512,1024]{1,0:T(8,128)(2,1)S(1)} %copy-done.5, ...), kind=kOutput, calls=%fused_computation.16 | convolution fusion | flops 686424064 | bytes 2629632 | tf_op jit(solution)/shard_map/dot_general | solution.py:117
  191.1 3.6 %all-to-all-start.3 = ((bf16[32,128,128]{2,1,0:T(8,128)(2,1)}), bf16[32,128,128]{2,1,0:T(8,128)(2,1)S(1)}, u32[]{:S(2)}, u32[]{:S(2)}) async-start(bf16[32,128,128]{2,1,0:T(8,128)(2,1)} %bitcast.98), calls=%async_computation.3 | async-start | bytes 2097152 | tf_op jit(solution)/shard_map/all_to_all | solution.py:28
  194.8 27.4 %all-to-all-done.3 = bf16[32,128,128]{2,1,0:T(8,128)(2,1)S(1)} async-done(((bf16[32,128,128]{2,1,0:T(8,128)(2,1)}), bf16[32,128,128]{2,1,0:T(8,128)(2,1)S(1)}, u32[]{:S(2)}, u32[]{:S(2)}) %all-to-all-start.3) | async-done | bytes 1048608 | tf_op jit(solution)/shard_map/all_to_all | solution.py:28
  222.2 24.6 %scatter_custom_fusion.2 = f32[8192,128]{1,0:T(8,128)} fusion(s32[4096]{0:T(1024)S(1)} %bitcast.109, bf16[4096,128]{1,0:T(8,128)(2,1)S(1)} %bitcast.94, f32[]{:T(128)} %constant.16.clone.1), kind=kCustom, calls=%fused_computation.18 | custom fusion | flops 1048576 | bytes 5242884 | tf_op jit(solution)/shard_map/scatter-add | solution.py:125
  (58 shorter events, 3.2 us)
Async XLA Ops:
  7.2 131.0 %copy-start = (bf16[1024,1024]{1,0:T(8,128)(2,1)S(1)}, bf16[1024,1024]{1,0:T(8,128)(2,1)}, u32[]{:S(2)}) copy-start(bf16[1024,1024]{1,0:T(8,128)(2,1)} %param.21) | copy-start | bytes 6291460
  8.3 10.6 %copy-start.11 = (s32[512,4]{0,1:T(4,128)S(1)}, s32[512,4]{0,1:T(4,128)}, u32[]{:S(2)}) copy-start(s32[512,4]{0,1:T(4,128)} %param.14) | copy-start | bytes 24580
  56.4 30.1 %all-to-all-start.1 = ((bf16[32,128,128]{2,1,0:T(8,128)(2,1)}), bf16[32,128,128]{2,1,0:T(8,128)(2,1)S(1)}, u32[]{:S(2)}, u32[]{:S(2)}) async-start(bf16[32,128,128]{2,1,0:T(8,128)(2,1)} %select_convert_fusion), calls=%async_computation.1 | async-start | bytes 2097152 | tf_op jit(solution)/shard_map/all_to_all | solution.py:28
  59.0 72.1 %all-gather.2.cloned.1.call-start = ((), (), s32[]{:S(2)}) async-start(), calls=%async_computation.4 | async-start | bytes 1179648 | tf_op jit(solution)/shard_map/all_gather | solution.py:76
  86.5 1.0 copy-start.7
  87.5 5.4 %copy-start.12 = (s32[4,4]{1,0:T(4,128)S(1)}, s32[4,4]{1,0:T(4,128)}, u32[]{:S(2)}) copy-start(s32[4,4]{1,0:T(4,128)} %param.16) | copy-start | bytes 196
  87.5 5.4 %copy-start.13 = (s32[4,4]{1,0:T(4,128)S(1)}, s32[4,4]{1,0:T(4,128)}, u32[]{:S(2)}) copy-start(s32[4,4]{1,0:T(4,128)} %param.15) | copy-start | bytes 196
  87.5 5.5 %copy-start.14 = (bf16[1024]{0:T(1024)(128)(2,1)S(1)}, bf16[1024]{0:T(1024)(128)(2,1)}, u32[]{:S(2)}) copy-start(bf16[1024]{0:T(1024)(128)(2,1)} %param.22) | copy-start | bytes 6148
  87.5 5.5 %copy-start.1 = (bf16[4,4,128,128]{3,2,1,0:T(8,128)(2,1)S(1)}, bf16[4,4,128,128]{3,2,1,0:T(8,128)(2,1)}, u32[]{:S(2)}) copy-start(bf16[4,4,128,128]{3,2,1,0:T(8,128)(2,1)} %param.17) | copy-start | bytes 1572868
  87.5 6.0 %copy-start.6 = (bf16[128,1024]{1,0:T(8,128)(2,1)S(1)}, bf16[128,1024]{1,0:T(8,128)(2,1)}, u32[]{:S(2)}) copy-start(bf16[128,1024]{1,0:T(8,128)(2,1)} %param.18) | copy-start | bytes 786436
  93.3 3.1 %copy-start.2 = (bf16[1024,1024]{1,0:T(8,128)(2,1)S(1)}, bf16[1024,1024]{1,0:T(8,128)(2,1)}, u32[]{:S(2)}) copy-start(bf16[1024,1024]{1,0:T(8,128)(2,1)} %param.20) | copy-start | bytes 6291460
  138.1 1.3 copy-start.3
  138.1 1.3 copy-start.9
  138.2 1.3 copy-start.10
  143.0 1.3 copy-start.4
  145.6 3.6 %copy-start.8 = (bf16[128,1024]{1,0:T(8,128)(2,1)S(1)}, bf16[128,1024]{1,0:T(8,128)(2,1)}, u32[]{:S(2)}) copy-start(bf16[128,1024]{1,0:T(8,128)(2,1)} %convolution_convert_fusion.1) | copy-start | bytes 786436
  157.2 28.0 %copy-start.5 = (bf16[512,1024]{1,0:T(8,128)(2,1)S(1)}, bf16[512,1024]{1,0:T(8,128)(2,1)}, u32[]{:S(2)}) copy-start(bf16[512,1024]{1,0:T(8,128)(2,1)} %copy-done.4) | copy-start | bytes 3145732
  191.1 31.1 %all-to-all-start.3 = ((bf16[32,128,128]{2,1,0:T(8,128)(2,1)}), bf16[32,128,128]{2,1,0:T(8,128)(2,1)S(1)}, u32[]{:S(2)}, u32[]{:S(2)}) async-start(bf16[32,128,128]{2,1,0:T(8,128)(2,1)} %bitcast.98), calls=%async_computation.3 | async-start | bytes 2097152 | tf_op jit(solution)/shard_map/all_to_all | solution.py:28
Sparse Core Ops, SparseCore 0:
  93.0 38.0 all-gather.1

commit v2 on v1

v2 whole, which is shorter than its diff:
```python
import jax
import jax.numpy as jnp
from jax import lax
from jax.experimental import pallas as pl
from jax.experimental.pallas import tpu as pltpu
from jax.sharding import PartitionSpec as P

EPSILON = 1e-06
LANES = 128
GROUP = 16

VMEM = pltpu.VMEM
SMEM = pltpu.SMEM


def call(kernel, outs, ins_space, args, scratch=(), flops=0):
    single = not isinstance(outs, (list, tuple))
    out_list = [outs] if single else list(outs)
    result = pl.pallas_call(
        kernel,
        out_shape=out_list,
        in_specs=[pl.BlockSpec(memory_space=space) for space in ins_space],
        out_specs=[pl.BlockSpec(memory_space=VMEM) for _ in out_list],
        scratch_shapes=list(scratch),
        cost_estimate=pl.CostEstimate(flops=flops, transcendentals=0, bytes_accessed=1 << 20),
    )(*args)
    return result[0] if single else result


def dot(left, right, left_dim, right_dim):
    return lax.dot_general(
        left, right, (((left_dim,), (right_dim,)), ((), ())), preferred_element_type=jnp.float32
    )


def ones_where(mask):
    return jnp.where(mask, 1.0, 0.0).astype(jnp.bfloat16)


def route_kernel(owner_ref, row_ref, request_ref, place_ref):
    lookups, nodes = owner_ref.shape
    devices, capacity = request_ref.shape
    owners = lax.broadcasted_iota(jnp.int32, (devices, nodes), 0)
    earlier = ones_where(
        lax.broadcasted_iota(jnp.int32, (nodes, nodes), 0)
        < lax.broadcasted_iota(jnp.int32, (nodes, nodes), 1)
    )
    hits = [owner_ref[j : j + 1, :] == owners for j in range(lookups)]
    before = dot(jnp.concatenate([ones_where(hit) for hit in hits], axis=0), earlier, 1, 0)
    carry = jnp.zeros((devices, 1), jnp.float32)
    place = jnp.zeros((devices, nodes), jnp.float32)
    slots = lax.broadcasted_iota(jnp.int32, (capacity, nodes), 0).astype(jnp.float32)
    high, low, taken = [], [], []
    for j in range(lookups):
        position = before[j * devices : (j + 1) * devices, :] + carry
        carry = carry + jnp.sum(jnp.where(hits[j], 1.0, 0.0), axis=1, keepdims=True)
        place = place + jnp.where(hits[j], position + 1.0, 0.0)
        own = jnp.sum(jnp.where(hits[j], position, 0.0), axis=0, keepdims=True)
        taken.append(ones_where(own == slots))
        row = row_ref[j : j + 1, :] + 1
        upper = (row >> 7).astype(jnp.float32)
        lower = (row & 127).astype(jnp.float32)
        high.append(jnp.where(hits[j], upper, 0.0).astype(jnp.bfloat16))
        low.append(jnp.where(hits[j], lower, 0.0).astype(jnp.bfloat16))
    taken = jnp.concatenate(taken, axis=1)
    request = dot(jnp.concatenate(high, axis=1), taken, 1, 1) * 128.0 + dot(
        jnp.concatenate(low, axis=1), taken, 1, 1
    )
    request_ref[...] = request.astype(jnp.int32)
    place_ref[...] = place.astype(jnp.int32) - 1


def fetch_kernel(id_ref, table_ref, out_ref, rows_ref):
    chunks = out_ref.shape[0] // LANES
    rows_ref[...] = jnp.zeros(rows_ref.shape, jnp.float32)

    def step(chunk, _):
        for group in range(LANES // GROUP):
            base = chunk * LANES + group * GROUP

            @pl.when(id_ref[base] > 0)
            def _():
                for i in range(GROUP):
                    row = jnp.maximum(id_ref[base + i] - 1, 0)
                    rows_ref[pl.ds(group * GROUP + i, 1), :] = table_ref[pl.ds(row, 1), :]

        start = pl.multiple_of(chunk * LANES, LANES)
        out_ref[pl.ds(start, LANES), :] = rows_ref[...].astype(jnp.bfloat16)
        return 0

    lax.fori_loop(0, chunks, step, 0)


def select_rows(place_ref, first, count, capacity):
    nodes = place_ref.shape[1]
    slots = lax.broadcasted_iota(jnp.int32, (capacity, nodes), 0)
    parts = [ones_where(place_ref[o : o + 1, :] == slots) for o in range(first, first + count)]
    return jnp.concatenate(parts, axis=0)


def combine_kernel(place_ref, returned_ref, feature_ref):
    devices = place_ref.shape[0]
    capacity = returned_ref.shape[0] // devices
    count = max(1, 512 // capacity)
    total = None
    for first in range(0, devices, count):
        chosen = select_rows(place_ref, first, count, capacity)
        rows = returned_ref[first * capacity : (first + count) * capacity, :]
        part = dot(rows, chosen, 0, 0)
        total = part if total is None else total + part
    feature_ref[...] = total.T.astype(jnp.bfloat16)


def spread_kernel(place_ref, d_self_ref, back_ref, out_ref):
    devices = place_ref.shape[0]
    capacity = out_ref.shape[0] // devices
    count = max(1, 512 // capacity)
    total = d_self_ref[...]
    for source in range(back_ref.shape[0]):
        total = total + back_ref[source].astype(jnp.float32)
    d_feature = total.astype(jnp.bfloat16)
    for first in range(0, devices, count):
        chosen = select_rows(place_ref, first, count, capacity)
        out_ref[first * capacity : (first + count) * capacity, :] = dot(
            chosen, d_feature, 1, 0
        ).astype(jnp.bfloat16)


def deposit_kernel(id_ref, ids_ref, grad_ref, out_ref, sums_ref):
    chunks = ids_ref.shape[0]

    def clear(i, _):
        start = pl.multiple_of(i * 256, 256)
        out_ref[pl.ds(start, 256), :] = jnp.zeros((256, out_ref.shape[1]), jnp.float32)
        return 0

    lax.fori_loop(0, out_ref.shape[0] // 256, clear, 0)
    rows = jnp.maximum(ids_ref[...] - 1, 0).astype(jnp.float32)
    columns = rows.T
    same_group = (
        lax.broadcasted_iota(jnp.int32, (LANES, LANES), 0) // GROUP
        == lax.broadcasted_iota(jnp.int32, (LANES, LANES), 1) // GROUP
    )
    for chunk in range(chunks):
        same = (columns[:, chunk : chunk + 1] == rows[chunk : chunk + 1, :]) & same_group
        sums_ref[chunk * LANES : (chunk + 1) * LANES, :] = dot(
            ones_where(same), grad_ref[chunk * LANES : (chunk + 1) * LANES, :], 1, 0
        )

    def step(chunk, _):
        for group in range(LANES // GROUP):
            base = chunk * LANES + group * GROUP

            @pl.when(id_ref[base] > 0)
            def _():
                targets = [jnp.maximum(id_ref[base + i] - 1, 0) for i in range(GROUP)]
                fresh = [
                    out_ref[pl.ds(targets[i], 1), :] + sums_ref[pl.ds(base + i, 1), :]
                    for i in range(GROUP)
                ]
                for i in range(GROUP):
                    out_ref[pl.ds(targets[i], 1), :] = fresh[i]

        return 0

    lax.fori_loop(0, chunks, step, 0)


def sage_kernel(
    index_ref,
    gathered_ref,
    feature_ref,
    adjacency_ref,
    map_pool_ref,
    map_self_ref,
    w_neigh_ref,
    gain_ref,
    cotangent_ref,
    node_out_ref,
    d_self_ref,
    owed_ref,
    slope_ref,
    mean_ref,
    inverse_ref,
    pre_ref,
    d_pre_ref,
    d_mean_ref,
    total_ref,
):
    blocks, fanout, block_rows, _ = adjacency_ref.shape
    nodes, hidden = pre_ref.shape
    span = fanout * block_rows

    def wide(block):
        return jnp.concatenate([adjacency_ref[block, k] for k in range(fanout)], axis=1)

    def forward(block, _):
        sources = jnp.concatenate(
            [gathered_ref[index_ref[block * fanout + k]] for k in range(fanout)], axis=0
        )
        start = pl.multiple_of(block * span, span)
        pooled_pre = dot(sources, map_pool_ref[...], 1, 0)
        gate = 1.0 / (1.0 + jnp.exp(-pooled_pre))
        pooled = (pooled_pre * gate).astype(jnp.bfloat16)
        slope_ref[pl.ds(start, span), :] = gate * (1.0 + pooled_pre * (1.0 - gate))
        weights = wide(block)
        inverse = 1.0 / jnp.sum(weights.astype(jnp.float32), axis=1, keepdims=True)
        own = pl.multiple_of(block * block_rows, block_rows)
        inverse_ref[pl.ds(own, block_rows), :] = jnp.broadcast_to(inverse, (block_rows, LANES))
        mean_ref[pl.ds(own, block_rows), :] = (dot(weights, pooled, 1, 0) * inverse).astype(
            jnp.bfloat16
        )
        return 0

    lax.fori_loop(0, blocks, forward, 0)
    pre_ref[...] = dot(feature_ref[...], map_self_ref[...], 1, 0) + dot(
        mean_ref[...], w_neigh_ref[...], 1, 0
    )
    gain = gain_ref[...].astype(jnp.float32)
    piece = 64

    def middle(part, _):
        start = pl.multiple_of(part * piece, piece)
        here = pl.ds(start, piece)
        pre_act = pre_ref[here, :]
        gate = 1.0 / (1.0 + jnp.exp(-pre_act))
        active = pre_act * gate
        scale = lax.rsqrt(jnp.mean(active * active, axis=1, keepdims=True) + EPSILON)
        node_out_ref[here, :] = (active * scale * gain).astype(jnp.bfloat16)
        weighted = gain * cotangent_ref[here, :].astype(jnp.float32)
        shift = (scale * scale * scale) * jnp.mean(weighted * active, axis=1, keepdims=True)
        d_active = scale * weighted - active * shift
        d_pre_ref[here, :] = (d_active * (gate * (1.0 + pre_act * (1.0 - gate)))).astype(
            jnp.bfloat16
        )
        return 0

    lax.fori_loop(0, nodes // piece, middle, 0)
    d_pre = d_pre_ref[...]
    d_self_ref[...] = dot(d_pre, map_self_ref[...], 1, 1)
    d_mean_ref[...] = dot(d_pre, w_neigh_ref[...], 1, 1)
    total_ref[...] = jnp.zeros(total_ref.shape, jnp.float32)

    def backward(block, _):
        own = pl.multiple_of(block * block_rows, block_rows)
        inverse = inverse_ref[pl.ds(own, block_rows), :][:, :1]
        d_scaled = (d_mean_ref[pl.ds(own, block_rows), :] * inverse).astype(jnp.bfloat16)
        start = pl.multiple_of(block * span, span)
        share = dot(wide(block), d_scaled, 0, 0)
        d_pool = (share * slope_ref[pl.ds(start, span), :]).astype(jnp.bfloat16)
        d_source = dot(d_pool, map_pool_ref[...], 1, 1)
        for k in range(fanout):
            target = index_ref[block * fanout + k]
            total_ref[target] += d_source[k * block_rows : (k + 1) * block_rows, :]
        return 0

    lax.fori_loop(0, blocks, backward, 0)
    owed_ref[...] = total_ref[...].astype(jnp.bfloat16)


def swap_all(buffer):
    return lax.all_to_all(buffer, ("table", "dom"), split_axis=0, concat_axis=0, tiled=True)


def body(
    tables,
    owner_ids,
    row_ids,
    neighbour_part,
    neighbour_block,
    adjacency,
    w_in,
    w_pool,
    w_self,
    w_neigh,
    out_gain,
    cotangent,
):
    groups = lax.axis_size("table")
    domains = lax.axis_size("dom")
    devices = groups * domains
    node_count, lookup_count = owner_ids.shape
    table_width = tables.shape[2]
    rows_local = tables.shape[1]
    hidden = w_self.shape[0]
    block_rows = adjacency.shape[-1]
    block_count = node_count // block_rows
    fanout = neighbour_part.shape[1]
    capacity = max(2, (2 * node_count * lookup_count + devices - 1) // devices)
    slot_count = devices * capacity
    chunks = slot_count // LANES
    f32, bf16 = jnp.float32, jnp.bfloat16

    map_pool = jnp.dot(w_in, w_pool, preferred_element_type=f32).astype(bf16)
    map_self = jnp.dot(w_in, w_self, preferred_element_type=f32).astype(bf16)

    requests, place = call(
        route_kernel,
        [
            jax.ShapeDtypeStruct((devices, capacity), jnp.int32),
            jax.ShapeDtypeStruct((devices, node_count), jnp.int32),
        ],
        [VMEM, VMEM],
        (owner_ids.T, row_ids.T),
    )
    incoming = swap_all(requests)
    flat_ids = incoming.reshape(-1)
    fetched = call(
        fetch_kernel,
        jax.ShapeDtypeStruct((slot_count, table_width), bf16),
        [SMEM, VMEM],
        (flat_ids, tables[0]),
        scratch=[pltpu.VMEM((LANES, table_width), f32)],
    )
    returned = swap_all(fetched.reshape(devices, capacity, table_width))
    feature = call(
        combine_kernel,
        jax.ShapeDtypeStruct((node_count, table_width), bf16),
        [VMEM, VMEM],
        (place, returned.reshape(slot_count, table_width)),
    )
    gathered = lax.all_to_all(
        jnp.broadcast_to(feature[None], (domains, node_count, table_width)),
        "dom",
        split_axis=0,
        concat_axis=0,
        tiled=True,
    )
    flat_index = neighbour_part.reshape(-1) * block_count + neighbour_block.reshape(-1)
    node_out, d_self, owed = call(
        sage_kernel,
        [
            jax.ShapeDtypeStruct((node_count, hidden), bf16),
            jax.ShapeDtypeStruct((node_count, table_width), f32),
            jax.ShapeDtypeStruct((domains * block_count, block_rows, table_width), bf16),
        ],
        [SMEM] + [VMEM] * 8,
        (
            flat_index,
            gathered.reshape(domains * block_count, block_rows, table_width),
            feature,
            adjacency,
            map_pool,
            map_self,
            w_neigh,
            out_gain.reshape(1, hidden),
            cotangent,
        ),
        scratch=[
            pltpu.VMEM((node_count * fanout, hidden), f32),
            pltpu.VMEM((node_count, hidden), bf16),
            pltpu.VMEM((node_count, LANES), f32),
            pltpu.VMEM((node_count, hidden), f32),
            pltpu.VMEM((node_count, hidden), bf16),
            pltpu.VMEM((node_count, hidden), f32),
            pltpu.VMEM((domains * block_count, block_rows, table_width), f32),
        ],
        flops=5 * 10**9,
    )
    back = lax.all_to_all(
        owed.reshape(domains, node_count, table_width),
        "dom",
        split_axis=0,
        concat_axis=0,
        tiled=True,
    )
    outgoing = call(
        spread_kernel,
        jax.ShapeDtypeStruct((slot_count, table_width), bf16),
        [VMEM, VMEM, VMEM],
        (place, d_self, back),
    )
    owed_rows = swap_all(outgoing.reshape(devices, capacity, table_width))
    table_grad = call(
        deposit_kernel,
        jax.ShapeDtypeStruct((rows_local, table_width), f32),
        [SMEM, VMEM, VMEM],
        (flat_ids, flat_ids.reshape(chunks, LANES), owed_rows.reshape(slot_count, table_width)),
        scratch=[pltpu.VMEM((slot_count, table_width), f32)],
    )
    return (node_out, table_grad[None])


def solution(mesh):
    both = P(("table", "dom"), None)
    placed = (
        P("table", "dom", None),
        both,
        both,
        both,
        both,
        P(("table", "dom"), None, None, None),
        P(),
        P(),
        P(),
        P(),
        P(),
        both,
    )
    return jax.shard_map(
        body,
        mesh=mesh,
        in_specs=placed,
        out_specs=(both, P("table", "dom", None)),
        check_vma=False,
    )
```

time: 254 us -> 188 us (0.74); the launches traced: 254 us -> 185 us
  blocking collectives: 41.4 us -> 107 us
  waiting for transfers between devices: 87.8 us -> 22.3 us
  other arithmetic: 47.9 us -> 0.01 us
  Pallas kernels: 0 us -> 44.2 us
  local copies, waits for them, and re-layouts: 29.9 us -> 4.26 us
  matrix products: 26 us -> 2.32 us
  between operations: 14.4 us -> 0.69 us
  starting transfers between devices: 6.31 us -> 3.56 us
    all_to_all x1 -> x3, blocking collectives: 14.3 us -> 77.5 us  [swap_all(): lax.all_to_all(buffer, ('table', 'dom'), split_axis=0, concat_axis=0, til...]
    pallas_call x0 -> x6, Pallas kernels: none -> 44.2 us  [call(): pl.pallas_call(kernel, out_shape=out_list, in_specs=[pl.BlockSpec(memory_...]
    all_gather x1 -> x0, waiting for transfers between devices: 33.5 us -> none  [body(): gathered = lax.all_gather(feature, 'dom', axis=0, tiled=True)]
    all_to_all x2 -> x1, waiting for transfers between devices: 54.3 us -> 22.3 us  [body(): lax.all_to_all(jnp.broadcast_to(feature[None], (domains, node_count, tabl...]
    scatter-add x2 -> x0, other arithmetic: 28 us -> none  [the longest x1 24.6 us: body(): table_grad = jnp.zeros((rows_local, table_width), jnp.float32).at[grad_ro...]
    dot_general x10 -> x2, matrix products: 24.7 us -> 2.32 us  [the longest x1 1.16 us: body(): map_self = jnp.dot(w_in, w_self, preferred_element_type=f32).astype(bf16)]
    gather x2 -> x0, local copies, waits for them, and re-layouts: 15.8 us -> none  [the longest x1 13.2 us: body(): tables[0][safe_rows]]
    another operation x3 -> x0, other arithmetic: 9.41 us -> none
  transfers between devices with their start and end apart: 3 -> 1, of which waited for: 3 -> 1; matrix products, arithmetic and copies ran while one was open for 2% -> 2% of each run, Pallas kernels for 0% -> 0%
where the time goes in v2:
time: 188 us; the launch traced here: 185 us
  blocking collectives  107 us (57%)
  Pallas kernels  44.2 us (24%)
  waiting for transfers between devices  22.3 us (12%)
  local copies, waits for them, and re-layouts  4.26 us (2%)
  starting transfers between devices  3.56 us (2%)
  matrix products  2.32 us (1%)
    all_to_all x3, blocking collectives, swap_all(): lax.all_to_all(buffer, ('table', 'dom'), split_axis=0, concat_axis=0, til...  77.5 us
    pallas_call x6, Pallas kernels, call(): pl.pallas_call(kernel, out_shape=out_list, in_specs=[pl.BlockSpec(memory_...  44.2 us
    all_to_all x1, blocking collectives, body(): lax.all_to_all(owed.reshape(domains, node_count, table_width), 'dom', spl...  29.7 us
    all_to_all x1, waiting for transfers between devices, body(): lax.all_to_all(jnp.broadcast_to(feature[None], (domains, node_count, tabl...  22.3 us
  transfers between devices with their start and end apart: 1, of which 1 were waited for; matrix products, arithmetic and copies ran while one was open for 2% of the time, Pallas kernels for 0%

profile of v2, /device:TPU:0, one launch (start us, length us, event | category | flops | bytes accessed | tf_op | source)
XLA Modules:
  0.0 184.6 jit_solution(16957791545057156048)
XLA Ops:
  0.6 0.0 copy-start
  0.6 2.2 %shard_map.131 = (s32[32,128]{1,0:T(8,128)}, s32[32,512]{1,0:T(8,128)}) custom-call(s32[4,512]{1,0:T(4,128)} %bitcast.31, s32[4,512]{1,0:T(4,128)} %bitcast.32), custom_call_target="tpu_custom_call" | custom-call | bytes 1048576 | tf_op jit(solution)/shard_map/pallas_call | solution.py:19
  2.8 14.4 %all_to_all.31 = s32[32,1,128]{2,1,0:T(1,128)} all-to-all(s32[32,1,128]{2,1,0:T(1,128)} %bitcast.30), channel_id=1, replica_groups=mesh['table'=4,'dom'=8] {'table','dom'}, dimensions={0} | all-to-all | bytes 32768 | tf_op jit(solution)/shard_map/all_to_all | solution.py:262
  17.2 8.3 %shard_map.132 = bf16[4096,128]{1,0:T(8,128)(2,1)} custom-call(s32[4096]{0:T(1024)} %bitcast.27, f32[8192,128]{1,0:T(8,128)} %bitcast.19), custom_call_target="tpu_custom_call" | custom-call | bytes 1048576 | tf_op jit(solution)/shard_map/pallas_call | solution.py:19
  25.4 32.0 %all_to_all.32 = bf16[32,128,128]{2,1,0:T(8,128)(2,1)} all-to-all(bf16[32,128,128]{2,1,0:T(8,128)(2,1)} %bitcast.22), channel_id=1, replica_groups=mesh['table'=4,'dom'=8] {'table','dom'}, dimensions={0} | all-to-all | bytes 2097152 | tf_op jit(solution)/shard_map/all_to_all | solution.py:262
  57.4 0.0 copy-start.4
  57.4 0.0 copy-start.5
  57.4 0.0 copy-start.6
  57.4 0.0 copy-start.2
  57.4 2.8 %shard_map.133.feature_ref = bf16[512,128]{1,0:T(8,128)(2,1)} custom-call(s32[32,512]{1,0:T(8,128)} %get-tuple-element.7.place_ref, bf16[4096,128]{1,0:T(8,128)(2,1)} %bitcast.24), custom_call_target="tpu_custom_call" | custom-call | bytes 1048576 | tf_op jit(solution)/shard_map/pallas_call | solution.py:19
  60.3 2.0 %broadcast_in_dim.4 = bf16[8,512,128]{2,1,0:T(8,128)(2,1)} broadcast(bf16[512,128]{1,0:T(8,128)(2,1)} %shard_map.133.feature_ref), dimensions={1,2} | broadcast | bytes 1179648 | tf_op jit(solution)/shard_map/broadcast_in_dim | solution.py:323
  62.3 3.6 %all-to-all-start.2 = ((bf16[8,512,128]{2,1,0:T(8,128)(2,1)}), bf16[8,512,128]{2,1,0:T(8,128)(2,1)S(1)}, u32[]{:S(2)}, u32[]{:S(2)}) async-start(bf16[8,512,128]{2,1,0:T(8,128)(2,1)} %broadcast_in_dim.4), calls=%async_computation.2 | async-start | bytes 2097152 | tf_op jit(solution)/shard_map/all_to_all | solution.py:322
  65.8 0.0 copy-done.4
  65.9 0.0 copy-done.5
  65.9 0.7 add.6.index_ref
  66.5 0.0 copy-done.6
  66.5 0.0 copy-start.1
  66.5 0.6 reshape.41.gain_ref
  67.1 0.0 copy-done
  67.1 0.0 copy-done.2
  67.1 1.2 convolution_convert_fusion.1.map_pool_ref
  68.3 0.0 copy-done.1
  68.3 1.2 convolution_convert_fusion.map_self_ref
  69.5 22.3 %all-to-all-done.2 = bf16[8,512,128]{2,1,0:T(8,128)(2,1)S(1)} async-done(((bf16[8,512,128]{2,1,0:T(8,128)(2,1)}), bf16[8,512,128]{2,1,0:T(8,128)(2,1)S(1)}, u32[]{:S(2)}, u32[]{:S(2)}) %all-to-all-start.2) | async-done | bytes 1048608 | tf_op jit(solution)/shard_map/all_to_all | solution.py:322
  91.7 0.0 copy-start.3
  91.7 1.0 copy-done.3
  92.7 16.7 %shard_map.134 = (bf16[512,1024]{1,0:T(8,128)(2,1)}, f32[512,128]{1,0:T(8,128)}, bf16[32,128,128]{2,1,0:T(8,128)(2,1)}) custom-call(s32[16]{0:T(128)} %add.6.index_ref, bf16[32,128,128]{2,1,0:T(8,128)(2,1)} %bitcast.25, bf16[512,128]{1,0:T(8,128)(2,1)} %shard_map.133.feature_ref, bf16[4,4,128,128]{3,2,1,0:T(8,128)(2,1)} %adjacency_ref.1, ...), custom_call_target="tpu_custom_call" | custom-call | flops 5000000000 | bytes 1048576 | tf_op jit(solution)/shard_map/pallas_call | solution.py:19
  109.4 29.7 %all_to_all.33.back_ref = bf16[8,512,128]{2,1,0:T(8,128)(2,1)} all-to-all(bf16[8,512,128]{2,1,0:T(8,128)(2,1)} %bitcast.26), channel_id=1, replica_groups=mesh['table'=4,'dom'=8] {'dom'}, dimensions={0} | all-to-all | bytes 2097152 | tf_op jit(solution)/shard_map/all_to_all | solution.py:360
  139.1 3.6 %shard_map.135 = bf16[4096,128]{1,0:T(8,128)(2,1)} custom-call(s32[32,512]{1,0:T(8,128)} %get-tuple-element.7.place_ref, f32[512,128]{1,0:T(8,128)} %get-tuple-element.10.d_self_ref, bf16[8,512,128]{2,1,0:T(8,128)(2,1)} %all_to_all.33.back_ref), custom_call_target="tpu_custom_call" | custom-call | bytes 1048576 | tf_op jit(solution)/shard_map/pallas_call | solution.py:19
  142.8 31.2 %all_to_all.34 = bf16[32,128,128]{2,1,0:T(8,128)(2,1)} all-to-all(bf16[32,128,128]{2,1,0:T(8,128)(2,1)} %bitcast.23), channel_id=1, replica_groups=mesh['table'=4,'dom'=8] {'table','dom'}, dimensions={0} | all-to-all | bytes 2097152 | tf_op jit(solution)/shard_map/all_to_all | solution.py:262
  174.0 10.6 %shard_map.136 = f32[8192,128]{1,0:T(8,128)} custom-call(s32[4096]{0:T(1024)} %bitcast.28, s32[32,128]{1,0:T(8,128)} %bitcast.29, bf16[4096,128]{1,0:T(8,128)(2,1)} %bitcast.21), custom_call_target="tpu_custom_call" | custom-call | bytes 1048576 | tf_op jit(solution)/shard_map/pallas_call | solution.py:19
  (1 shorter events, 0.0 us)
Async XLA Ops:
  0.6 66.5 %copy-start = (bf16[1024,1024]{1,0:T(8,128)(2,1)S(1)}, bf16[1024,1024]{1,0:T(8,128)(2,1)}, u32[]{:S(2)}) copy-start(bf16[1024,1024]{1,0:T(8,128)(2,1)} %param.19) | copy-start | bytes 6291460
  57.4 8.4 %copy-start.4 = (s32[4,4]{1,0:T(4,128)S(1)}, s32[4,4]{1,0:T(4,128)}, u32[]{:S(2)}) copy-start(s32[4,4]{1,0:T(4,128)} %param.16) | copy-start | bytes 196
  57.4 8.4 %copy-start.5 = (s32[4,4]{1,0:T(4,128)S(1)}, s32[4,4]{1,0:T(4,128)}, u32[]{:S(2)}) copy-start(s32[4,4]{1,0:T(4,128)} %param.15) | copy-start | bytes 196
  57.4 9.1 %copy-start.6 = (bf16[1024]{0:T(1024)(128)(2,1)S(1)}, bf16[1024]{0:T(1024)(128)(2,1)}, u32[]{:S(2)}) copy-start(bf16[1024]{0:T(1024)(128)(2,1)} %param.22) | copy-start | bytes 6148
  57.4 9.7 %copy-start.2 = (bf16[128,1024]{1,0:T(8,128)(2,1)S(1)}, bf16[128,1024]{1,0:T(8,128)(2,1)}, u32[]{:S(2)}) copy-start(bf16[128,1024]{1,0:T(8,128)(2,1)} %param.18) | copy-start | bytes 786436
  62.3 29.4 %all-to-all-start.2 = ((bf16[8,512,128]{2,1,0:T(8,128)(2,1)}), bf16[8,512,128]{2,1,0:T(8,128)(2,1)S(1)}, u32[]{:S(2)}, u32[]{:S(2)}) async-start(bf16[8,512,128]{2,1,0:T(8,128)(2,1)} %broadcast_in_dim.4), calls=%async_computation.2 | async-start | bytes 2097152 | tf_op jit(solution)/shard_map/all_to_all | solution.py:322
  66.5 1.8 copy-start.1
  91.7 1.0 copy-start.3
